TPU v7x, 32 devices: a whole 2x2x4 slice. The times are simulated.
32 devices in a mesh: row: 8 (over y, x, core), col: 4 (over z).
Axes of the slice: x: 2, y: 2, z: 4, core: 2. Of those that a mesh axis runs over, the one named last changes fastest.
Arguments:
- jacobian: float32 [2, 4096, 256], P(None, ('row', 'col')), may hold values from -0.25 to 0.25
Outputs:
- normal_tiles: float32 [8, 2, 4, 512, 512], P('row', None, 'col')
All inputs are finite; a program needn't handle non-finite values.
Results may differ from a plain program's by a relative error of at most 0.0003.
Values sent between devices are 32-bit elements; how exact they have to be, the bound alone decides.
A program may use at most 64 MiB of HBM per device.

v0:
```python
import jax
import jax.numpy as jnp
from jax import lax
from jax.sharding import PartitionSpec as P


def from_partner(block, axis, distance):
    count = lax.axis_size(axis)
    route = []
    for low in range(count):
        high = low | 1 << distance
        if high != low and high < count:
            route += [(low, high), (high, low)]
    return lax.ppermute(block, axis, route)


def partner_rows(block, bit_number):
    return from_partner(block, ("row", "col"), bit_number)


def body(jacobian):
    row_index = lax.axis_index("row")
    col_index = lax.axis_index("col")
    col_count = lax.axis_size("col")
    cycles = lax.axis_size("row") // col_count
    panel_count = jacobian.shape[0]
    width = jacobian.shape[2]
    own_tile = lax.all_gather(jacobian, "col", axis=1, tiled=True)
    tile_size = own_tile.shape[1]
    col_bits = col_count.bit_length() - 1
    low_row = row_index % col_count
    moved = jacobian
    for bit_number in range(col_bits):
        first = partner_rows(moved, bit_number)
        second = partner_rows(first, bit_number + col_bits)
        differ = low_row >> bit_number & 1 != col_index >> bit_number & 1
        moved = jnp.where(differ, second, moved)
    gathered = lax.all_gather(moved, "row", axis=1, tiled=True)
    gathered = gathered.reshape(panel_count, cycles, tile_size, width)
    partners = [gathered[:, turn_index] for turn_index in range(cycles)]

    def product(partner):
        return jnp.einsum("pak,pbk->ab", own_tile, partner, precision=lax.Precision.HIGHEST)

    def empty_tile(partner):
        return jnp.zeros((tile_size, tile_size), jnp.float32)

    results = []
    for turn_index in range(cycles):
        column_tile = col_index + col_count * turn_index
        results.append(
            lax.cond(column_tile <= row_index, product, empty_tile, partners[turn_index])
        )
    blocks = jnp.stack(results, 0)
    return blocks[None, :, None]


def solution(mesh):
    in_specs = (P(None, ("row", "col"), None),)
    out_specs = P("row", None, "col", None, None)
    return jax.shard_map(body, mesh=mesh, in_specs=in_specs, out_specs=out_specs, check_vma=False)
```

profile of v0, /device:TPU:4, one launch (start us, length us, event | category | flops | bytes accessed | tf_op | source)
XLA Modules:
  0.0 115.7 jit_solution(6772489944896085306)
XLA Ops:
  6.5 0.0 all-gather.3.cloned.1.call-start
  6.5 1.6 %collective-permute-start = (f32[2,128,256]{2,1,0:T(8,128)}, f32[2,128,256]{2,1,0:T(8,128)S(1)}, u32[]{:S(2)}, u32[]{:S(2)}) collective-permute-start(f32[2,128,256]{2,1,0:T(8,128)} %param.5), channel_id=1, source_target_pairs={{0,1},{1,0},{2,3},{3,2},{4,5},{5,4},{6,7},{7,6},{8,9},{9,8},{10,11... | collective-permute-start | bytes 786440 | tf_op jit(solution)/shard_map/ppermute | solution.py:14
  8.1 6.7 %collective-permute-done = f32[2,128,256]{2,1,0:T(8,128)S(1)} collective-permute-done((f32[2,128,256]{2,1,0:T(8,128)}, f32[2,128,256]{2,1,0:T(8,128)S(1)}, u32[]{:S(2)}, u32[]{:S(2)}) %collective-permute-start) | collective-permute-done | bytes 262176 | tf_op jit(solution)/shard_map/ppermute | solution.py:14
  14.8 0.0 collective-permute-start.1
  14.8 1.5 %collective-permute-done.1 = f32[2,128,256]{2,1,0:T(8,128)S(1)} collective-permute-done((f32[2,128,256]{2,1,0:T(8,128)S(1)}, f32[2,128,256]{2,1,0:T(8,128)S(1)}, u32[]{:S(2)}, u32[]{:S(2)}) %collective-permute-start.1) | collective-permute-done | bytes 262176 | tf_op jit(solution)/shard_map/ppermute | solution.py:14
  16.3 1.0 broadcast_select_fusion
  17.3 2.7 %collective-permute-start.2 = (f32[2,128,256]{2,1,0:T(8,128)S(1)}, f32[2,128,256]{2,1,0:T(8,128)S(1)}, u32[]{:S(2)}, u32[]{:S(2)}) collective-permute-start(f32[2,128,256]{2,1,0:T(8,128)S(1)} %broadcast_select_fusion), channel_id=1, source_target_pairs={{0,2},{2,0},{1,3},{3,1},{4,6},{6,4},{5,7},{7,5},{8,10},{10,8},{9,1... | collective-permute-start | bytes 786440 | tf_op jit(solution)/shard_map/ppermute | solution.py:14
  20.0 11.3 %collective-permute-done.2 = f32[2,128,256]{2,1,0:T(8,128)S(1)} collective-permute-done((f32[2,128,256]{2,1,0:T(8,128)S(1)}, f32[2,128,256]{2,1,0:T(8,128)S(1)}, u32[]{:S(2)}, u32[]{:S(2)}) %collective-permute-start.2) | collective-permute-done | bytes 262176 | tf_op jit(solution)/shard_map/ppermute | solution.py:14
  31.3 1.5 %collective-permute-start.3 = (f32[2,128,256]{2,1,0:T(8,128)S(1)}, f32[2,128,256]{2,1,0:T(8,128)S(1)}, u32[]{:S(2)}, u32[]{:S(2)}) collective-permute-start(f32[2,128,256]{2,1,0:T(8,128)S(1)} %collective-permute-done.2), channel_id=1, source_target_pairs={{0,8},{8,0},{1,9},{9,1},{2,10},{10,2},{3,11},{11,3},{4,12},{12,4},... | collective-permute-start | bytes 786440 | tf_op jit(solution)/shard_map/ppermute | solution.py:14
  32.8 5.1 %collective-permute-done.3 = f32[2,128,256]{2,1,0:T(8,128)S(1)} collective-permute-done((f32[2,128,256]{2,1,0:T(8,128)S(1)}, f32[2,128,256]{2,1,0:T(8,128)S(1)}, u32[]{:S(2)}, u32[]{:S(2)}) %collective-permute-start.3) | collective-permute-done | bytes 262176 | tf_op jit(solution)/shard_map/ppermute | solution.py:14
  37.8 0.7 broadcast_select_fusion.1
  38.6 0.0 all-gather.3.cloned.1.call-update
  38.6 0.0 all-gather.5.cloned.1.call-start
  38.7 0.7 all-gather.5.cloned.1.call-update
  39.4 30.0 %all-gather.3.cloned.1.call-done = f32[2,1024,256]{2,1,0:T(8,128)} async-done(((f32[2,128,256]{2,1,0:T(8,128)}), f32[2,1024,256]{2,1,0:T(8,128)}) %all-gather.3.cloned.1.call-update) | async-done | bytes 2097168 | tf_op jit(solution)/shard_map/all_gather | solution.py:38
  69.3 1.7 %copy.2 = f32[2,2,512,256]{3,2,0,1:T(8,128)S(1)} copy(f32[2,2,512,256]{3,2,1,0:T(8,128)} %bitcast.17) | data formatting | bytes 4194304 | tf_op jit(solution)/shard_map/cond | solution.py:52
  71.1 27.9 %all-gather.5.cloned.1.call-done = f32[2,512,256]{2,1,0:T(8,128)} async-done(((f32[2,128,256]{2,1,0:T(8,128)}), f32[2,512,256]{2,1,0:T(8,128)}) %all-gather.5.cloned.1.call-update) | async-done | bytes 1048592 | tf_op jit(solution)/shard_map/all_gather | solution.py:28
  99.0 3.1 %conditional.3 = (f32[1,512,512]{2,1,0:T(8,128)S(1)}) conditional(s32[]{:T(128)} %convert_element_type.7, () %tuple.23, (f32[2,2,512,256]{3,2,0,1:T(8,128)S(1)}, f32[2,512,256]{2,1,0:T(8,128)}) %tuple.24), branch_computations={%region_2.3_spmd, %region_3.4_spmd} | conditional | flops 1610612736 | bytes 3145736 | solution.py:52
  99.0 3.1 %convolution_bitcast_fusion.1 = f32[1,512,512]{2,1,0:T(8,128)S(1)} fusion(f32[2,512,256]{2,1,0:T(8,128)} %get-tuple-element.27, f32[2,2,512,256]{3,2,0,1:T(8,128)S(1)} %get-tuple-element.28), kind=kOutput, calls=%fused_computation.3 | convolution fusion | flops 1610612736 | bytes 3145728 | tf_op jit(solution)/shard_map/cond/branch_1_fun/pak,pbk->ab/dot_general | solution.py:43
  102.1 4.1 %conditional.2 = (f32[1,512,512]{2,1,0:T(8,128)}) conditional(s32[]{:T(128)} %convert_element_type.6, () %tuple.21, (f32[2,2,512,256]{3,2,0,1:T(8,128)S(1)}, f32[2,512,256]{2,1,0:T(8,128)}) %tuple.24), branch_computations={%region_0.1_spmd, %region_1.2_spmd} | conditional | flops 1610612736 | bytes 3145736 | solution.py:52
  102.1 4.1 %convolution_bitcast_fusion = f32[1,512,512]{2,1,0:T(8,128)} fusion(f32[2,512,256]{2,1,0:T(8,128)} %get-tuple-element.25, f32[2,2,512,256]{3,2,0,1:T(8,128)S(1)} %get-tuple-element.26), kind=kOutput, calls=%fused_computation | convolution fusion | flops 1610612736 | bytes 3145728 | tf_op jit(solution)/shard_map/cond/branch_1_fun/pak,pbk->ab/dot_general | solution.py:43
  106.2 2.7 %maximum_bitcast_fusion = f32[1,2,1,512,512]{4,3,2,1,0:T(8,128)} fusion(f32[1,512,512]{2,1,0:T(8,128)S(1)} %get-tuple-element.34, f32[1,512,512]{2,1,0:T(8,128)} %get-tuple-element.33), kind=kLoop, calls=%fused_computation.6 | loop fusion | flops 524288 | bytes 4194304 | tf_op jit(solution)/shard_map/broadcast_in_dim | solution.py:55
Async XLA Ops:
  6.5 62.8 %all-gather.3.cloned.1.call-start = ((), (), s32[]{:S(2)}) async-start(), calls=%async_computation | async-start | bytes 2359296 | tf_op jit(solution)/shard_map/all_gather | solution.py:38
  6.5 8.3 %collective-permute-start = (f32[2,128,256]{2,1,0:T(8,128)}, f32[2,128,256]{2,1,0:T(8,128)S(1)}, u32[]{:S(2)}, u32[]{:S(2)}) collective-permute-start(f32[2,128,256]{2,1,0:T(8,128)} %param.5), channel_id=1, source_target_pairs={{0,1},{1,0},{2,3},{3,2},{4,5},{5,4},{6,7},{7,6},{8,9},{9,8},{10,11... | collective-permute-start | bytes 786440 | tf_op jit(solution)/shard_map/ppermute | solution.py:14
  14.8 1.5 %collective-permute-start.1 = (f32[2,128,256]{2,1,0:T(8,128)S(1)}, f32[2,128,256]{2,1,0:T(8,128)S(1)}, u32[]{:S(2)}, u32[]{:S(2)}) collective-permute-start(f32[2,128,256]{2,1,0:T(8,128)S(1)} %collective-permute-done), channel_id=1, source_target_pairs={{0,4},{4,0},{1,5},{5,1},{2,6},{6,2},{3,7},{7,3},{8,12},{12,8},{9,1... | collective-permute-start | bytes 786440 | tf_op jit(solution)/shard_map/ppermute | solution.py:14
  17.3 14.0 %collective-permute-start.2 = (f32[2,128,256]{2,1,0:T(8,128)S(1)}, f32[2,128,256]{2,1,0:T(8,128)S(1)}, u32[]{:S(2)}, u32[]{:S(2)}) collective-permute-start(f32[2,128,256]{2,1,0:T(8,128)S(1)} %broadcast_select_fusion), channel_id=1, source_target_pairs={{0,2},{2,0},{1,3},{3,1},{4,6},{6,4},{5,7},{7,5},{8,10},{10,8},{9,1... | collective-permute-start | bytes 786440 | tf_op jit(solution)/shard_map/ppermute | solution.py:14
  31.3 6.5 %collective-permute-start.3 = (f32[2,128,256]{2,1,0:T(8,128)S(1)}, f32[2,128,256]{2,1,0:T(8,128)S(1)}, u32[]{:S(2)}, u32[]{:S(2)}) collective-permute-start(f32[2,128,256]{2,1,0:T(8,128)S(1)} %collective-permute-done.2), channel_id=1, source_target_pairs={{0,8},{8,0},{1,9},{9,1},{2,10},{10,2},{3,11},{11,3},{4,12},{12,4},... | collective-permute-start | bytes 786440 | tf_op jit(solution)/shard_map/ppermute | solution.py:14
  38.6 60.4 %all-gather.5.cloned.1.call-start = ((), (), s32[]{:S(2)}) async-start(), calls=%async_computation.1 | async-start | bytes 1310720 | tf_op jit(solution)/shard_map/all_gather | solution.py:28
Sparse Core Ops, SparseCore 0:
  38.7 30.5 all-gather.2
  70.9 28.0 all-gather.4
where the time goes:
time: 116 us
  waiting for transfers between devices  83.2 us (72%)
  between operations  13.4 us (12%)
  matrix products  7.14 us (6%)
  starting transfers between devices  5.77 us (5%)
  other arithmetic  4.43 us (4%)
  local copies, waits for them, and re-layouts  1.73 us (1%)
    all_gather x1, waiting for transfers between devices, body(): gathered = lax.all_gather(moved, 'row', axis=1, tiled=True)  30 us
    all_gather x1, waiting for transfers between devices, body(): own_tile = lax.all_gather(jacobian, 'col', axis=1, tiled=True)  27.9 us
    ppermute x4, waiting for transfers between devices, from_partner(): return lax.ppermute(block, axis, route)  24.6 us
    dot_general x2, matrix products, product(): jnp.einsum('pak,pbk->ab', own_tile, partner, precision=lax.Precision.HIGH...  7.14 us
    ppermute x4, starting transfers between devices, from_partner(): return lax.ppermute(block, axis, route)  5.72 us
    broadcast_in_dim x1, other arithmetic, body(): return blocks[None, :, None]  2.71 us
  transfers between devices with their start and end apart: 6, of which 6 were waited for; matrix products, arithmetic and copies ran while one was open for 1% of the time, Pallas kernels for 0%

commit v1 on v0

v1 whole, which is shorter than its diff:
```python
import functools

import jax
import jax.numpy as jnp
from jax import lax
from jax.experimental import pallas as pl
from jax.experimental.pallas import tpu as pltpu
from jax.sharding import PartitionSpec as P

SPLIT = 1
MESH = pl.DeviceIdType.MESH


def flip(index, bit):
    size = 1 << bit
    return index + (1 - 2 * (index // size % 2)) * size


def kernel(row_count, col_count, x_hbm, out, own, cols, left, right,
           in_sem, z_send, z_recv, c_send, c_recv, barrier_go):
    row = lax.axis_index("row")
    col = lax.axis_index("col")
    turns = row_count // col_count
    panels, height, width = own.shape[1:]
    piece = height // SPLIT
    pieces = [(p, pl.ds(h * piece, piece)) for p in range(panels) for h in range(SPLIT)]
    bits = (row_count // 2).bit_length() - 1
    parity = row % 2
    sibling = flip(row, 0)
    sign = 2 * parity - 1
    carrier = parity == col % 2

    load = pltpu.make_async_copy(x_hbm, own.at[col], in_sem)
    load.start()

    barrier = pltpu.get_barrier_semaphore()

    def greet(r, c):
        pl.semaphore_signal(barrier, inc=1, device_id={"row": r, "col": c}, device_id_type=MESH)

    for bit in range(bits + 1):
        greet(flip(row, bit), col)

    @pl.when(col > 0)
    def _():
        greet(row, col - 1)

    @pl.when(col < col_count - 1)
    def _():
        greet(row, col + 1)

    peers = bits + 1 + (col > 0).astype(jnp.int32) + (col < col_count - 1).astype(jnp.int32)
    pl.semaphore_wait(barrier, peers)
    load.wait()

    def along(phase):
        return sign if phase == 0 else -sign

    def line_copy(phase, step, k):
        to = col + along(phase)
        origin = col - along(phase) * step
        part = own.at[origin, pieces[k][0], pieces[k][1]]
        return pltpu.make_async_remote_copy(
            src_ref=part, dst_ref=part,
            send_sem=z_send.at[phase, step, k], recv_sem=z_recv.at[origin, k],
            device_id={"row": row, "col": to}, device_id_type=MESH)

    def origin_ok(phase, step):
        origin = col - along(phase) * step
        return (origin >= 0) & (origin < col_count)

    def target_ok(phase):
        to = col + along(phase)
        return (to >= 0) & (to < col_count)

    def tile_copy(turn, origin, k, bit, from_own):
        where = (pieces[k][0], pieces[k][1])
        landing = cols.at[(turn, origin) + where]
        source = own.at[(origin,) + where] if from_own else landing
        return pltpu.make_async_remote_copy(
            src_ref=source, dst_ref=landing,
            send_sem=c_send.at[turn, origin, k, bit], recv_sem=c_recv.at[turn, origin, k],
            device_id={"row": flip(row, bit), "col": col}, device_id_type=MESH)

    def distance(turn):
        home = (col + col_count * turn) // 2
        chip = row // 2
        d = 0
        for bit in range(bits):
            low = chip // (1 << bit) % 2
            far = home // (1 << bit) % 2
            d = d + (low + far) % 2 * (1 << bit)
        return d

    distances = [distance(turn) for turn in range(turns)]
    at_home = row % col_count == col
    home_turn = row // col_count
    away = [row != col + col_count * turn for turn in range(turns)]

    def spread(turn, origin, k):
        for bit in reversed(range(bits)):
            @pl.when(distances[turn] < (1 << bit))
            def _(bit=bit):
                tile_copy(turn, origin, k, bit + 1, False).start()
        tile_copy(turn, origin, k, 0, False).start()

    def line_step(phase, step):
        @pl.when(origin_ok(phase, step))
        def _():
            origin = col - along(phase) * step
            for k in range(len(pieces)):
                if step > 0:
                    line_copy(phase, step, k).wait_recv()

                @pl.when(target_ok(phase))
                def _(k=k):
                    line_copy(phase, step, k).start()

                if phase == 0 or step > 0:
                    @pl.when(at_home)
                    def _(k=k):
                        for bit in reversed(range(bits + 1)):
                            tile_copy(home_turn, origin, k, bit, True).start()

    def tile_step(phase, step):
        @pl.when(origin_ok(phase, step) & carrier)
        def _():
            origin = col - along(phase) * step
            for k in range(len(pieces)):
                for turn in range(turns):
                    @pl.when(away[turn])
                    def _(turn=turn, k=k):
                        tile_copy(turn, origin, k, 0, False).wait_recv()
                        spread(turn, origin, k)

    def line_drain(phase):
        @pl.when(target_ok(phase))
        def _():
            for step in range(col_count):
                @pl.when(origin_ok(phase, step))
                def _(step=step):
                    for k in range(len(pieces)):
                        line_copy(phase, step, k).wait_send()

    def swap():
        line_drain(0)
        pl.semaphore_signal(barrier_go, inc=1, device_id={"row": sibling, "col": col},
                            device_id_type=MESH)
        pl.semaphore_wait(barrier_go, 1)

    steps = [(0, step) for step in range(col_count)] + [(1, step) for step in range(col_count)]
    behind = []
    for phase, step in steps:
        if phase == 1 and step == 0:
            swap()
        line_step(phase, step)
        if len(behind) > 0:
            tile_step(*behind.pop(0))
        if phase == 0 or step > 0:
            behind.append((phase, step))
    for item in behind:
        tile_step(*item)

    line_drain(1)

    def each_origin(origin, carry):
        for turn in range(turns):
            for k in range(len(pieces)):
                @pl.when(carrier)
                def _(turn=turn, k=k):
                    for bit in range(bits):
                        @pl.when(distances[turn] < (1 << bit))
                        def _(bit=bit):
                            tile_copy(turn, origin, k, bit + 1, False).wait_send()
                    tile_copy(turn, origin, k, 0, False).wait_send()

                @pl.when(jnp.logical_not(carrier))
                def _(turn=turn, k=k):
                    tile_copy(turn, origin, k, 0, False).wait_recv()
        return carry

    lax.fori_loop(0, col_count, each_origin, 0)

    depth = panels * width

    def fill(target, block, places):
        for origin in range(col_count):
            for p in range(panels):
                value = block[origin, p]
                high = value.astype(jnp.bfloat16)
                low = (value - high.astype(jnp.float32)).astype(jnp.bfloat16)
                for place, half in enumerate(places):
                    target[pl.ds(origin * height, height), pl.ds(place * depth + p * width, width)] = (
                        high if half == 0 else low)

    fill(left, own, (0, 0, 1))
    for turn in range(turns):
        tile = col + col_count * turn

        @pl.when(tile > row)
        def _(turn=turn):
            out[turn] = jnp.zeros(out.shape[1:], jnp.float32)

        @pl.when(tile <= row)
        def _(turn=turn):
            @pl.when(jnp.logical_not(away[turn]))
            def _():
                fill(right, own, (0, 1, 0))

            @pl.when(away[turn])
            def _():
                fill(right, cols.at[turn], (0, 1, 0))

            out[turn] = lax.dot_general(left[...], right[...], (((1,), (1,)), ((), ())),
                                        preferred_element_type=jnp.float32)


def body(jacobian):
    row_count = lax.axis_size("row")
    col_count = lax.axis_size("col")
    turns = row_count // col_count
    panels, height, width = jacobian.shape
    tile = height * col_count
    pieces = panels * SPLIT
    bits = (row_count // 2).bit_length() - 1
    dma = pltpu.SemaphoreType.DMA
    blocks = pl.pallas_call(
        functools.partial(kernel, row_count, col_count),
        out_shape=jax.ShapeDtypeStruct((turns, tile, tile), jnp.float32),
        in_specs=[pl.BlockSpec(memory_space=pl.ANY)],
        out_specs=pl.BlockSpec(memory_space=pltpu.VMEM),
        scratch_shapes=[
            pltpu.VMEM((col_count, panels, height, width), jnp.float32),
            pltpu.VMEM((turns, col_count, panels, height, width), jnp.float32),
            pltpu.VMEM((tile, 3 * panels * width), jnp.bfloat16),
            pltpu.VMEM((tile, 3 * panels * width), jnp.bfloat16),
            dma,
            dma((2, col_count, pieces)),
            dma((col_count, pieces)),
            dma((turns, col_count, pieces, bits + 1)),
            dma((turns, col_count, pieces)),
            pltpu.SemaphoreType.REGULAR,
        ],
        compiler_params=pltpu.CompilerParams(collective_id=0, has_side_effects=True),
    )(jacobian)
    return blocks[None, :, None]


def solution(mesh):
    in_specs = (P(None, ("row", "col"), None),)
    out_specs = P("row", None, "col", None, None)
    return jax.shard_map(body, mesh=mesh, in_specs=in_specs, out_specs=out_specs, check_vma=False)
```

time: 116 us -> 89.2 us (0.77)
  the two profiles are of different devices: /device:TPU:4 before, /device:TPU:17 now
where the time goes in v1:
time: 89.2 us; the launch traced here: 89.1 us
  Pallas kernels  86 us (96%)
  local copies, waits for them, and re-layouts  3.08 us (3%)
    pallas_call x1, Pallas kernels, body(): pl.pallas_call(functools.partial(kernel, row_count, col_count), out_shape...  86 us
    unnamed x1, local copies, waits for them, and re-layouts  3.08 us

profile of v1, /device:TPU:17, one launch (start us, length us, event | category | flops | bytes accessed | tf_op | source)
XLA Modules:
  0.0 89.1 jit_solution(9375331920678057355)
XLA Ops:
  0.0 86.0 %shard_map.17 = f32[2,512,512]{2,1,0:T(8,128)} custom-call(f32[2,128,256]{2,1,0:T(8,128)} %x_hbm.1), custom_call_target="tpu_custom_call" | custom-call | tf_op jit(solution)/shard_map/pallas_call | solution.py:227
  86.0 3.1 %copy.4 = f32[1,2,1,512,512]{4,3,2,1,0:T(8,128)} copy(f32[1,2,1,512,512]{4,3,2,1,0:T(8,128)} %bitcast.3) | data formatting | bytes 4194304

commit v2 on v1

--- a/solution.py
+++ b/solution.py
@@ -7,7 +7,9 @@
 from jax.experimental.pallas import tpu as pltpu
 from jax.sharding import PartitionSpec as P
 
-SPLIT = 1
+SPLIT = 2
+RELAY_LAG = 1
+LEAF_LAG = 2
 MESH = pl.DeviceIdType.MESH
 
 
@@ -17,7 +19,7 @@
 
 
 def kernel(row_count, col_count, x_hbm, out, own, cols, left, right,
-           in_sem, z_send, z_recv, c_send, c_recv, barrier_go):
+           in_sem, z_send, z_recv, c_send, c_recv):
     row = lax.axis_index("row")
     col = lax.axis_index("col")
     turns = row_count // col_count
@@ -26,7 +28,6 @@
     pieces = [(p, pl.ds(h * piece, piece)) for p in range(panels) for h in range(SPLIT)]
     bits = (row_count // 2).bit_length() - 1
     parity = row % 2
-    sibling = flip(row, 0)
     sign = 2 * parity - 1
     carrier = parity == col % 2
 
@@ -122,16 +123,22 @@
                         for bit in reversed(range(bits + 1)):
                             tile_copy(home_turn, origin, k, bit, True).start()
 
-    def tile_step(phase, step):
-        @pl.when(origin_ok(phase, step) & carrier)
+    relays = [carrier & away[turn] & (distances[turn] < (1 << (bits - 1))) for turn in range(turns)]
+    leaves = [carrier & (distances[turn] >= (1 << (bits - 1))) for turn in range(turns)]
+
+    def tile_step(phase, step, roles):
+        @pl.when(origin_ok(phase, step))
         def _():
             origin = col - along(phase) * step
             for k in range(len(pieces)):
                 for turn in range(turns):
-                    @pl.when(away[turn])
+                    @pl.when(roles[turn])
                     def _(turn=turn, k=k):
                         tile_copy(turn, origin, k, 0, False).wait_recv()
-                        spread(turn, origin, k)
+                        if roles is relays:
+                            spread(turn, origin, k)
+                        else:
+                            tile_copy(turn, origin, k, 0, False).start()
 
     def line_drain(phase):
         @pl.when(target_ok(phase))
@@ -142,25 +149,18 @@
                     for k in range(len(pieces)):
                         line_copy(phase, step, k).wait_send()
 
-    def swap():
-        line_drain(0)
-        pl.semaphore_signal(barrier_go, inc=1, device_id={"row": sibling, "col": col},
-                            device_id_type=MESH)
-        pl.semaphore_wait(barrier_go, 1)
-
-    steps = [(0, step) for step in range(col_count)] + [(1, step) for step in range(col_count)]
-    behind = []
-    for phase, step in steps:
-        if phase == 1 and step == 0:
-            swap()
-        line_step(phase, step)
-        if len(behind) > 0:
-            tile_step(*behind.pop(0))
-        if phase == 0 or step > 0:
-            behind.append((phase, step))
-    for item in behind:
-        tile_step(*item)
-
+    steps = [(0, step) for step in range(col_count)] + [(1, step) for step in range(1, col_count)]
+    for place in range(len(steps) + LEAF_LAG):
+        if place < len(steps):
+            line_step(*steps[place])
+            if steps[place] == (0, 0):
+                line_step(1, 0)
+        if 0 <= place - RELAY_LAG < len(steps):
+            tile_step(*steps[place - RELAY_LAG], relays)
+        if 0 <= place - LEAF_LAG < len(steps):
+            tile_step(*steps[place - LEAF_LAG], leaves)
+
+    line_drain(0)
     line_drain(1)
 
     def each_origin(origin, carry):
@@ -239,7 +239,6 @@
             dma((col_count, pieces)),
             dma((turns, col_count, pieces, bits + 1)),
             dma((turns, col_count, pieces)),
-            pltpu.SemaphoreType.REGULAR,
         ],
         compiler_params=pltpu.CompilerParams(collective_id=0, has_side_effects=True),
     )(jacobian)

time: 89.2 us -> 35.5 us (0.40)
  the two profiles are of different devices: /device:TPU:17 before, /device:TPU:3 now
where the time goes in v2:
time: 35.5 us; the launch traced here: 35.3 us
  Pallas kernels  32.2 us (91%)
  local copies, waits for them, and re-layouts  3.08 us (9%)
    pallas_call x1, Pallas kernels, body(): pl.pallas_call(functools.partial(kernel, row_count, col_count), out_shape...  32.2 us
    unnamed x1, local copies, waits for them, and re-layouts  3.08 us

profile of v2, /device:TPU:3, one launch (start us, length us, event | category | flops | bytes accessed | tf_op | source)
XLA Modules:
  0.0 35.3 jit_solution(18279373023067803498)
XLA Ops:
  0.0 32.2 %shard_map.17 = f32[2,512,512]{2,1,0:T(8,128)} custom-call(f32[2,128,256]{2,1,0:T(8,128)} %x_hbm.1), custom_call_target="tpu_custom_call" | custom-call | tf_op jit(solution)/shard_map/pallas_call | solution.py:227
  32.3 3.1 %copy.4 = f32[1,2,1,512,512]{4,3,2,1,0:T(8,128)} copy(f32[1,2,1,512,512]{4,3,2,1,0:T(8,128)} %bitcast.3) | data formatting | bytes 4194304

commit v3 on v2

--- a/solution.py
+++ b/solution.py
@@ -9,7 +9,7 @@
 
 SPLIT = 2
 RELAY_LAG = 1
-LEAF_LAG = 2
+LEAF_LAG = 4
 MESH = pl.DeviceIdType.MESH
 
 
@@ -19,7 +19,7 @@
 
 
 def kernel(row_count, col_count, x_hbm, out, own, cols, left, right,
-           in_sem, z_send, z_recv, c_send, c_recv):
+           in_sem, z_send, z_recv, c_send, c_recv, f_send):
     row = lax.axis_index("row")
     col = lax.axis_index("col")
     turns = row_count // col_count
@@ -42,6 +42,9 @@
     for bit in range(bits + 1):
         greet(flip(row, bit), col)
 
+    if bits == 2:
+        greet(flip(flip(row, 1), 2), col)
+
     @pl.when(col > 0)
     def _():
         greet(row, col - 1)
@@ -50,7 +53,7 @@
     def _():
         greet(row, col + 1)
 
-    peers = bits + 1 + (col > 0).astype(jnp.int32) + (col < col_count - 1).astype(jnp.int32)
+    peers = bits + 1 + (bits == 2) + (col > 0).astype(jnp.int32) + (col < col_count - 1).astype(jnp.int32)
     pl.semaphore_wait(barrier, peers)
     load.wait()
 
@@ -105,6 +108,16 @@
                 tile_copy(turn, origin, k, bit + 1, False).start()
         tile_copy(turn, origin, k, 0, False).start()
 
+    def direct(step):
+        return bits == 2 and step == col_count - 1
+
+    def far_copy(turn, origin, k):
+        where = (origin, pieces[k][0], pieces[k][1])
+        return pltpu.make_async_remote_copy(
+            src_ref=own.at[where], dst_ref=cols.at[(turn,) + where],
+            send_sem=f_send.at[k], recv_sem=c_recv.at[turn, origin, k],
+            device_id={"row": flip(flip(row, 1), 2), "col": col}, device_id_type=MESH)
+
     def line_step(phase, step):
         @pl.when(origin_ok(phase, step))
         def _():
@@ -120,6 +133,8 @@
                 if phase == 0 or step > 0:
                     @pl.when(at_home)
                     def _(k=k):
+                        if direct(step):
+                            far_copy(home_turn, origin, k).start()
                         for bit in reversed(range(bits + 1)):
                             tile_copy(home_turn, origin, k, bit, True).start()
 
@@ -135,7 +150,7 @@
                     @pl.when(roles[turn])
                     def _(turn=turn, k=k):
                         tile_copy(turn, origin, k, 0, False).wait_recv()
-                        if roles is relays:
+                        if roles is relays and not direct(step):
                             spread(turn, origin, k)
                         else:
                             tile_copy(turn, origin, k, 0, False).start()
@@ -149,7 +164,7 @@
                     for k in range(len(pieces)):
                         line_copy(phase, step, k).wait_send()
 
-    steps = [(0, step) for step in range(col_count)] + [(1, step) for step in range(1, col_count)]
+    steps = [(0, 0)] + [(phase, step) for step in range(1, col_count) for phase in (0, 1)]
     for place in range(len(steps) + LEAF_LAG):
         if place < len(steps):
             line_step(*steps[place])
@@ -163,24 +178,6 @@
     line_drain(0)
     line_drain(1)
 
-    def each_origin(origin, carry):
-        for turn in range(turns):
-            for k in range(len(pieces)):
-                @pl.when(carrier)
-                def _(turn=turn, k=k):
-                    for bit in range(bits):
-                        @pl.when(distances[turn] < (1 << bit))
-                        def _(bit=bit):
-                            tile_copy(turn, origin, k, bit + 1, False).wait_send()
-                    tile_copy(turn, origin, k, 0, False).wait_send()
-
-                @pl.when(jnp.logical_not(carrier))
-                def _(turn=turn, k=k):
-                    tile_copy(turn, origin, k, 0, False).wait_recv()
-        return carry
-
-    lax.fori_loop(0, col_count, each_origin, 0)
-
     depth = panels * width
 
     def fill(target, block, places):
@@ -195,11 +192,41 @@
 
     fill(left, own, (0, 0, 1))
     for turn in range(turns):
-        tile = col + col_count * turn
-
-        @pl.when(tile > row)
+        @pl.when(col + col_count * turn > row)
         def _(turn=turn):
             out[turn] = jnp.zeros(out.shape[1:], jnp.float32)
+
+    def each_origin(origin, carry):
+        for turn in range(turns):
+            for k in range(len(pieces)):
+                @pl.when(carrier)
+                def _(turn=turn, k=k):
+                    for bit in range(bits):
+                        passes = distances[turn] < (1 << bit)
+                        if bits == 2:
+                            far = (origin - col == col_count - 1) | (col - origin == col_count - 1)
+                            passes = passes & (jnp.logical_not(far) | (distances[turn] == 0))
+
+                        @pl.when(passes)
+                        def _(bit=bit):
+                            tile_copy(turn, origin, k, bit + 1, False).wait_send()
+                    tile_copy(turn, origin, k, 0, False).wait_send()
+
+                @pl.when(jnp.logical_not(carrier))
+                def _(turn=turn, k=k):
+                    tile_copy(turn, origin, k, 0, False).wait_recv()
+        return carry
+
+    lax.fori_loop(0, col_count, each_origin, 0)
+    if bits == 2:
+        @pl.when(at_home & ((col == 0) | (col == col_count - 1)))
+        def _():
+            for k in range(len(pieces)):
+                far_copy(home_turn, col_count - 1 - col, k).wait_send()
+
+
+    for turn in range(turns):
+        tile = col + col_count * turn
 
         @pl.when(tile <= row)
         def _(turn=turn):
@@ -239,6 +266,7 @@
             dma((col_count, pieces)),
             dma((turns, col_count, pieces, bits + 1)),
             dma((turns, col_count, pieces)),
+            dma((pieces,)),
         ],
         compiler_params=pltpu.CompilerParams(collective_id=0, has_side_effects=True),
     )(jacobian)

time: 35.5 us -> 34.6 us (0.975)
  Pallas kernels: 32.2 us -> 31.1 us
    pallas_call x1, Pallas kernels: 32.2 us -> 31.1 us  [body(): pl.pallas_call(functools.partial(kernel, row_count, col_count), out_shape...]
where the time goes in v3:
time: 34.6 us; the launch traced here: 34.2 us
  Pallas kernels  31.1 us (90%)
  local copies, waits for them, and re-layouts  3.08 us (9%)
    pallas_call x1, Pallas kernels, body(): pl.pallas_call(functools.partial(kernel, row_count, col_count), out_shape...  31.1 us
    unnamed x1, local copies, waits for them, and re-layouts  3.08 us

profile of v3, /device:TPU:3, one launch (start us, length us, event | category | flops | bytes accessed | tf_op | source)
XLA Modules:
  0.0 34.2 jit_solution(16398882437114149483)
XLA Ops:
  0.0 31.1 %shard_map.17 = f32[2,512,512]{2,1,0:T(8,128)} custom-call(f32[2,128,256]{2,1,0:T(8,128)} %x_hbm.1), custom_call_target="tpu_custom_call" | custom-call | tf_op jit(solution)/shard_map/pallas_call | solution.py:254
  31.1 3.1 %copy.4 = f32[1,2,1,512,512]{4,3,2,1,0:T(8,128)} copy(f32[1,2,1,512,512]{4,3,2,1,0:T(8,128)} %bitcast.3) | data formatting | bytes 4194304
